TPU v7x, 32 devices: a whole 2x2x4 slice. The times are simulated.
32 devices in a mesh: freq: 4 (over y, x), band: 8 (over z, core).
Axes of the slice: x: 2, y: 2, z: 4, core: 2. Of those that a mesh axis runs over, the one named last changes fastest.
Arguments:
- pair_density: bfloat16 [1024, 2, 8192], P(('freq', 'band')), may hold values from -6 to 6
- trial_vectors: bfloat16 [16, 2, 64, 8192], P('freq', None, None, 'band'), may hold values from -6 to 6
- frequency: float32 [16], P('freq'), may hold values from 0.05 to 20
- val_energy: float32 [32], replicated, may hold values from -3 to -0.1
- cond_energy: float32 [32], replicated, may hold values from 0.1 to 4
- pair_index: int32 [1024], P(('freq', 'band')), may hold values from 0 to 1023, each once
Outputs:
- images: float32 [16, 2, 64, 8192], P('freq', None, None, 'band')
- subspace: float32 [16, 2, 64, 64], P('freq')
Inputs may be any that keep to these rules, and one draw needn't show every extreme that they name: `pair_index`: every pair number 0 to 1023 appears exactly once.
All inputs are finite; a program needn't handle non-finite values.
Results may differ from a plain program's by a relative error of at most 0.0085.
Values may be sent and summed in bfloat16 or wider, within the bound.
No kernel may reach another device: no remote copies, remote signals or barrier semaphores. Data moves between devices by JAX's collectives and lax.ppermute only.
A program may use at most 128 MiB of HBM per device.

v0:
```python
import math
import jax
import jax.numpy as jnp
from jax import lax
from jax.sharding import PartitionSpec as P


def local_weights(pair_index, frequency, val_energy, cond_energy, prefactor):
    cond_count = cond_energy.shape[0]
    val_count = val_energy.shape[0]
    cond_pick = jnp.sum(
        jnp.where(
            (pair_index % cond_count)[:, None] == jnp.arange(cond_count)[None, :],
            cond_energy[None, :],
            0.0,
        ),
        axis=1,
    )
    val_pick = jnp.sum(
        jnp.where(
            (pair_index // cond_count)[:, None] == jnp.arange(val_count)[None, :],
            val_energy[None, :],
            0.0,
        ),
        axis=1,
    )
    delta = cond_pick - val_pick
    ratio = delta[:, None] / (
        delta[:, None] * delta[:, None] + frequency[None, :] * frequency[None, :]
    )
    return (-4.0 * prefactor * ratio).astype(jnp.bfloat16)


def crossing_terms(density, vectors):
    products = jnp.einsum("pcg,fekg->fcekp", density, vectors, preferred_element_type=jnp.float32)
    return jnp.stack(
        [products[:, 0, 0] + products[:, 1, 1], products[:, 0, 1] - products[:, 1, 0]], 1
    )


def scale_terms(crossings, weights):
    factor = jnp.transpose(weights.astype(jnp.float32))[:, None, None, :]
    return (factor * crossings).astype(jnp.bfloat16)


def mix_terms(scaled):
    scaled_real = scaled[:, 0]
    scaled_imag = scaled[:, 1]
    return jnp.stack(
        [jnp.stack([scaled_real, -scaled_imag], 1), jnp.stack([scaled_imag, scaled_real], 1)], 1
    )


def image_terms(density, mixed):
    return jnp.einsum("pcg,fdckp->fdkg", density, mixed, preferred_element_type=jnp.float32)


def shards(pair_density, trial_vectors, frequency, val_energy, cond_energy, pair_index):
    groups = lax.axis_size("freq")
    members = lax.axis_size("band")
    pair_count = pair_density.shape[0] * groups * members
    grid_count = trial_vectors.shape[3] * members
    prefactor = 1.0 / math.sqrt(2.0 * grid_count * pair_count)
    regrouped = lax.all_to_all(pair_density, "band", split_axis=2, concat_axis=0, tiled=True)
    grouped = lax.all_gather(regrouped, "freq", axis=0, tiled=True)
    all_index = lax.all_gather(pair_index, ("freq", "band"), axis=0, tiled=True)
    crossings = crossing_terms(grouped, trial_vectors)
    summed = lax.psum(crossings, "band")
    all_weights = local_weights(all_index, frequency, val_energy, cond_energy, prefactor)
    scaled = scale_terms(summed, all_weights)
    images = image_terms(grouped, mix_terms(scaled))
    vectors = trial_vectors.astype(jnp.float32)
    highest = lax.Precision.HIGHEST
    real_part = jnp.einsum(
        "fkg,flg->fkl", vectors[:, 0], images[:, 0], precision=highest
    ) + jnp.einsum("fkg,flg->fkl", vectors[:, 1], images[:, 1], precision=highest)
    imag_part = jnp.einsum(
        "fkg,flg->fkl", vectors[:, 0], images[:, 1], precision=highest
    ) - jnp.einsum("fkg,flg->fkl", vectors[:, 1], images[:, 0], precision=highest)
    partial_value = jnp.stack([real_part, imag_part], 1) / grid_count
    subspace = lax.psum(partial_value, "band")
    return (images, subspace)


def solution(mesh):
    return jax.shard_map(
        shards,
        mesh=mesh,
        in_specs=(
            P(("freq", "band"), None, None),
            P("freq", None, None, "band"),
            P("freq"),
            P(),
            P(),
            P(("freq", "band")),
        ),
        out_specs=(P("freq", None, None, "band"), P("freq", None, None, None)),
        check_vma=False,
    )
```

profile of v0, /device:TPU:0, one launch (start us, length us, event | category | flops | bytes accessed | tf_op | source)
XLA Modules:
  0.0 269.7 jit_solution(9058504637230988360)
XLA Ops:
  7.2 0.0 all-gather.2.cloned.1.call-start
  7.2 10.8 %copy.31 = bf16[32,2,8192]{0,1,2:T(2,128)(2,1)} copy(bf16[32,2,8192]{2,1,0:T(2,128)(2,1)} %param.6) | data formatting | bytes 2097152 | tf_op args[0]
  18.0 7.0 %reshape.101 = bf16[8,2,32768]{2,1,0:T(2,128)(2,1)S(1)} reshape(bf16[8192,2,32]{2,1,0:T(2,128)(2,1)} %bitcast.76) | data formatting | bytes 2097152
  24.9 32.7 %all_to_all.18 = bf16[8,2,32768]{2,1,0:T(2,128)(2,1)S(1)} all-to-all(bf16[8,2,32768]{2,1,0:T(2,128)(2,1)S(1)} %reshape.101), channel_id=1, replica_groups=mesh['freq'=4,'band'=8] {'band'}, dimensions={0} | all-to-all | bytes 2097152 | tf_op jit(solution)/shard_map/all_to_all | solution.py:64
  57.7 4.5 %reshape.102 = bf16[8192,2,32]{2,1,0:T(2,128)(2,1)} reshape(bf16[8,2,32768]{2,1,0:T(2,128)(2,1)S(1)} %all_to_all.18) | data formatting | bytes 2097152
  62.2 0.0 copy-start.1
  62.2 10.5 %copy.32 = bf16[32,2,8,1024]{3,0,2,1:T(8,128)(2,1)} copy(bf16[32,2,8,1024]{0,1,3,2:T(2,128)(2,1)} %bitcast.75) | data formatting | bytes 2097152 | tf_op jit(solution)/shard_map/all_to_all | solution.py:64
  72.6 0.0 all-gather.2.cloned.1.call-update
  72.6 0.0 all-reduce.4.cloned.1.call-start
  72.7 51.6 %all-gather.2.cloned.1.call-done = bf16[1024,2,1024]{2,0,1:T(8,128)(2,1)} async-done(((bf16[256,2,1024]{2,0,1:T(8,128)(2,1)}), bf16[1024,2,1024]{2,0,1:T(8,128)(2,1)}) %all-gather.2.cloned.1.call-update) | async-done | bytes 4194320 | tf_op jit(solution)/shard_map/all_gather | solution.py:65
  124.3 0.0 copy-done.1
  124.3 4.6 %fusion.4 = f32[4,2,2,64,1024]{4,3,1,2,0:T(8,128)S(1)} fusion(bf16[1024,2,1024]{2,0,1:T(8,128)(2,1)} %all-gather.2.cloned.1.call-done, bf16[4,2,64,1024]{3,2,1,0:T(8,128)(2,1)S(1)} %copy-done.1), kind=kOutput, calls=%fused_computation.4 | convolution fusion | flops 2147483648 | bytes 9437184 | tf_op jit(solution)/shard_map/pcg,fekg->fcekp/dot_general | solution.py:35
  128.9 0.1 fusion.15
  129.0 0.1 fusion.17
  129.2 1.5 pad_maximum_fusion
  130.6 0.0 copy-start.5
  130.6 0.0 copy-start.6
  130.6 0.0 copy-start.2
  130.6 0.0 copy-start.3
  130.6 0.0 all-reduce.4.cloned.1.call-update
  130.7 0.0 all-reduce.6.cloned.1.call-start
  130.7 0.6 copy-done.5
  131.3 0.0 copy-done.6
  131.3 0.2 dynamic-update-slice
  131.5 39.6 %all-reduce = s32[1024]{0:T(1024)S(1)} all-reduce(s32[1024]{0:T(1024)S(1)} %dynamic-update-slice), channel_id=1, replica_groups=mesh['freq'=4,'band'=8] {'freq','band'}, use_global_device_ids=true, to_apply=%add | all-reduce | flops 1024 | bytes 8192
  171.2 0.0 copy-done.2
  171.2 0.0 copy-done.3
  171.2 0.1 select_reduce_fusion
  171.3 0.1 fusion.29
  171.4 25.1 %all-reduce.4.cloned.1.call-done = f32[4,2,64,1024]{3,2,0,1:T(8,128)} async-done(((f32[4,2,64,1024]{3,2,0,1:T(8,128)}), f32[4,2,64,1024]{3,2,0,1:T(8,128)}) %all-reduce.4.cloned.1.call-update) | async-done | bytes 2097168 | tf_op jit(solution)/shard_map/psum | solution.py:68
  196.5 1.8 multiply_convert_fusion
  198.4 0.0 copy-start.4
  198.4 0.1 slice_negate_fusion
  198.5 0.2 maximum_bitcast_fusion
  198.7 1.9 copy-done.4
  200.5 2.3 fusion.8
  202.9 0.0 copy-start
  202.9 0.6 fusion.20
  203.5 0.6 fusion.19
  204.2 0.6 fusion.13
  204.8 0.0 copy-done
  204.8 0.6 fusion.14
  205.4 0.7 maximum_multiply_fusion
  206.2 0.0 all-reduce.6.cloned.1.call-update
  206.2 55.2 %all-reduce.6.cloned.1.call-done = f32[4,2,64,64]{2,3,0,1:T(8,128)} async-done(((f32[4,2,64,64]{2,3,0,1:T(8,128)}), f32[4,2,64,64]{2,3,0,1:T(8,128)}) %all-reduce.6.cloned.1.call-update) | async-done | bytes 131088 | tf_op jit(solution)/shard_map/psum | solution.py:81
  261.4 1.8 copy.38
  (4 shorter events, 0.0 us)
Async XLA Ops:
  7.2 117.1 %all-gather.2.cloned.1.call-start = ((), (), s32[]{:S(2)}) async-start(), calls=%async_computation.1 | async-start | bytes 5242880 | tf_op jit(solution)/shard_map/all_gather | solution.py:65
  62.2 62.2 %copy-start.1 = (bf16[4,2,64,1024]{3,2,1,0:T(8,128)(2,1)S(1)}, bf16[4,2,64,1024]{3,2,1,0:T(8,128)(2,1)}, u32[]{:S(2)}) copy-start(bf16[4,2,64,1024]{3,2,1,0:T(8,128)(2,1)} %param.7) | copy-start | bytes 3145732
  72.6 123.9 %all-reduce.4.cloned.1.call-start = ((), (), s32[]{:S(2)}) async-start(), calls=%async_computation.2 | async-start | bytes 4194304 | tf_op jit(solution)/shard_map/psum | solution.py:68
  130.6 0.7 copy-start.5
  130.6 0.7 copy-start.6
  130.6 40.6 %copy-start.2 = (f32[32]{0:T(128)S(1)}, f32[32]{0:T(128)}, u32[]{:S(2)}) copy-start(f32[32]{0:T(128)} %param.9) | copy-start | bytes 388
  130.6 40.6 %copy-start.3 = (f32[32]{0:T(128)S(1)}, f32[32]{0:T(128)}, u32[]{:S(2)}) copy-start(f32[32]{0:T(128)} %param.10) | copy-start | bytes 388
  130.7 130.8 %all-reduce.6.cloned.1.call-start = ((), (), s32[]{:S(2)}) async-start(), calls=%async_computation.3 | async-start | bytes 524288 | tf_op jit(solution)/shard_map/psum | solution.py:81
  198.4 2.2 copy-start.4
  202.9 1.9 copy-start
Sparse Core Ops, SparseCore 0:
  72.8 51.4 all-gather.1
  130.8 65.6 all-reduce.3
  206.3 55.0 all-reduce.5
where the time goes:
time: 271 us; the launch traced here: 270 us
  waiting for transfers between devices  132 us (49%)
  blocking collectives  72.4 us (27%)
  local copies, waits for them, and re-layouts  37.2 us (14%)
  between operations  13.9 us (5%)
  matrix products  9.4 us (3%)
  other arithmetic  4.8 us (2%)
    psum x1, waiting for transfers between devices, shards(): subspace = lax.psum(partial_value, 'band')  55.2 us
    all_gather x1, waiting for transfers between devices, shards(): grouped = lax.all_gather(regrouped, 'freq', axis=0, tiled=True)  51.6 us
    unnamed x1, blocking collectives  39.6 us
    all_to_all x1, blocking collectives, shards(): lax.all_to_all(pair_density, 'band', split_axis=2, concat_axis=0, tiled=T...  32.7 us
    unnamed x20, local copies, waits for them, and re-layouts  26.7 us
    psum x1, waiting for transfers between devices, shards(): summed = lax.psum(crossings, 'band')  25.1 us
    all_to_all x1, local copies, waits for them, and re-layouts, shards(): lax.all_to_all(pair_density, 'band', split_axis=2, concat_axis=0, tiled=T...  10.5 us
  transfers between devices with their start and end apart: 3, of which 3 were waited for; matrix products, arithmetic and copies ran while one was open for 0% of the time, Pallas kernels for 0%

commit v1 on v0

--- a/solution.py
+++ b/solution.py
@@ -3,6 +3,22 @@
 import jax.numpy as jnp
 from jax import lax
 from jax.sharding import PartitionSpec as P
+from jax.lax import axis_index, axis_size, ppermute
+
+
+def remake_array(array_here, at_axis, buf):
+    all_values, moved = (array_here.shape[:at_axis], array_here.shape[at_axis + 1 :])
+    g_now = jnp.moveaxis(array_here.reshape(*all_values, buf, -1, *moved), at_axis, 0)
+    return g_now
+
+
+def attach_halves(shard_in, out_dim):
+    shard_in = jnp.moveaxis(shard_in, 0, out_dim)
+    ready = shard_in.shape
+    newest = shard_in.reshape(
+        *ready[:out_dim], ready[out_dim] * ready[out_dim + 1], *ready[out_dim + 2 :]
+    )
+    return newest
 
 
 def local_weights(pair_index, frequency, val_energy, cond_energy, prefactor):
@@ -61,7 +77,21 @@
     pair_count = pair_density.shape[0] * groups * members
     grid_count = trial_vectors.shape[3] * members
     prefactor = 1.0 / math.sqrt(2.0 * grid_count * pair_count)
-    regrouped = lax.all_to_all(pair_density, "band", split_axis=2, concat_axis=0, tiled=True)
+
+    def paths_put(mine, comm_axis, page, s0):
+        u1, earlier = (axis_size(comm_axis), axis_index(comm_axis))
+        e_next = remake_array(mine, page, u1)
+        panels = [e_next[earlier]]
+        ix = 1
+        while ix < u1:
+            part_next = e_next[earlier ^ ix]
+            panels.append(ppermute(part_next, comm_axis, [(p, p ^ ix) for p in range(u1)]))
+            ix += 1
+        e_next = jnp.stack(panels, 0)[earlier ^ jnp.arange(u1)]
+        oldest = attach_halves(e_next, s0)
+        return oldest
+
+    regrouped = paths_put(pair_density, "band", 2, 0)
     grouped = lax.all_gather(regrouped, "freq", axis=0, tiled=True)
     all_index = lax.all_gather(pair_index, ("freq", "band"), axis=0, tiled=True)
     crossings = crossing_terms(grouped, trial_vectors)

time: 271 us -> 242 us (0.89)
  blocking collectives: 72.4 us -> 40.1 us
  local copies, waits for them, and re-layouts: 37.2 us -> 11.1 us
  waiting for transfers between devices: 132 us -> 152 us
  starting transfers between devices: 0.12 us -> 10.2 us
    all_to_all x1 -> x0, blocking collectives: 32.7 us -> none  [shards(): lax.all_to_all(pair_density, 'band', split_axis=2, concat_axis=0, tiled=T...]
    unnamed x20 -> x31, local copies, waits for them, and re-layouts: 26.7 us -> 5.18 us
    ppermute x0 -> x7, waiting for transfers between devices: none -> 13.6 us  [paths_put(): ppermute(part_next, comm_axis, [(p, p ^ ix) for p in range(u1)])]
    all_to_all x1 -> x0, local copies, waits for them, and re-layouts: 10.5 us -> none  [shards(): lax.all_to_all(pair_density, 'band', split_axis=2, concat_axis=0, tiled=T...]
    ppermute x0 -> x7, starting transfers between devices: none -> 10 us  [paths_put(): ppermute(part_next, comm_axis, [(p, p ^ ix) for p in range(u1)])]
    all_gather x1, waiting for transfers between devices: 51.6 us -> 58.3 us  [shards(): grouped = lax.all_gather(regrouped, 'freq', axis=0, tiled=True)]
  transfers between devices with their start and end apart: 3 -> 10, of which waited for: 3 -> 5; matrix products, arithmetic and copies ran while one was open for 0% -> 0% of each run, Pallas kernels for 0% -> 0%
where the time goes in v1:
time: 242 us
  waiting for transfers between devices  152 us (63%)
  blocking collectives  40.1 us (17%)
  between operations  14.1 us (6%)
  local copies, waits for them, and re-layouts  11.1 us (5%)
  starting transfers between devices  10.2 us (4%)
  matrix products  9.4 us (4%)
  other arithmetic  4.92 us (2%)
    all_gather x1, waiting for transfers between devices, shards(): grouped = lax.all_gather(regrouped, 'freq', axis=0, tiled=True)  58.3 us
    psum x1, waiting for transfers between devices, shards(): subspace = lax.psum(partial_value, 'band')  55.2 us
    unnamed x1, blocking collectives  40.1 us
    psum x1, waiting for transfers between devices, shards(): summed = lax.psum(crossings, 'band')  24.7 us
    ppermute x7, waiting for transfers between devices, paths_put(): ppermute(part_next, comm_axis, [(p, p ^ ix) for p in range(u1)])  13.6 us
    ppermute x7, starting transfers between devices, paths_put(): ppermute(part_next, comm_axis, [(p, p ^ ix) for p in range(u1)])  10 us
    unnamed x31, local copies, waits for them, and re-layouts  5.18 us
  transfers between devices with their start and end apart: 10, of which 5 were waited for; matrix products, arithmetic and copies ran while one was open for 0% of the time, Pallas kernels for 0%

profile of v1, /device:TPU:0, one launch (start us, length us, event | category | flops | bytes accessed | tf_op | source)
XLA Modules:
  0.0 241.6 jit_solution(8619679413355077814)
XLA Ops:
  7.2 0.0 all-gather.2.cloned.1.call-start
  7.2 1.8 reshape.148
  9.1 2.4 constant_dynamic-slice_fusion
  11.5 0.1 copy.105
  11.6 0.6 collective-permute-start
  12.2 0.1 copy.104
  12.2 2.6 %collective-permute-start.1 = (bf16[32,2,1024]{2,0,1:T(8,128)(2,1)S(1)}, bf16[32,2,1024]{2,0,1:T(8,128)(2,1)S(1)}, u32[]{:S(2)}, u32[]{:S(2)}) collective-permute-start(bf16[32,2,1024]{2,0,1:T(8,128)(2,1)S(1)} %bitcast.125), channel_id=1, source_target_pairs={{0,2},{1,3},{2,0},{3,1},{4,6},{5,7},{6,4},{7,5},{8,10},{9,11},{10,... | collective-permute-start | bytes 393224 | tf_op jit(solution)/shard_map/ppermute | solution.py:88
  14.9 0.1 copy.103
  15.0 0.2 collective-permute-start.2
  15.1 0.1 copy.102
  15.2 2.8 %collective-permute-start.3 = (bf16[32,2,1024]{2,0,1:T(8,128)(2,1)S(1)}, bf16[32,2,1024]{2,0,1:T(8,128)(2,1)S(1)}, u32[]{:S(2)}, u32[]{:S(2)}) collective-permute-start(bf16[32,2,1024]{2,0,1:T(8,128)(2,1)S(1)} %bitcast.122), channel_id=1, source_target_pairs={{0,4},{1,5},{2,6},{3,7},{4,0},{5,1},{6,2},{7,3},{8,12},{9,13},{10,... | collective-permute-start | bytes 393224 | tf_op jit(solution)/shard_map/ppermute | solution.py:88
  18.0 0.1 copy.101
  18.1 0.1 collective-permute-start.4
  18.2 0.1 fusion.29
  18.3 0.1 copy.100
  18.4 0.1 copy.99
  18.5 3.6 %collective-permute-start.5 = (bf16[32,2,1024]{2,0,1:T(8,128)(2,1)S(1)}, bf16[32,2,1024]{2,0,1:T(8,128)(2,1)S(1)}, u32[]{:S(2)}, u32[]{:S(2)}) collective-permute-start(bf16[32,2,1024]{2,0,1:T(8,128)(2,1)S(1)} %bitcast.124), channel_id=1, source_target_pairs={{0,6},{1,7},{2,4},{3,5},{4,2},{5,3},{6,0},{7,1},{8,14},{9,15},{10,... | collective-permute-start | bytes 393224 | tf_op jit(solution)/shard_map/ppermute | solution.py:88
  22.1 0.2 collective-permute-start.6
  22.3 4.2 %collective-permute-done.2 = bf16[32,2,1024]{2,0,1:T(8,128)(2,1)S(1)} collective-permute-done((bf16[32,2,1024]{2,0,1:T(8,128)(2,1)S(1)}, bf16[32,2,1024]{2,0,1:T(8,128)(2,1)S(1)}, u32[]{:S(2)}, u32[]{:S(2)}) %collective-permute-start.2) | collective-permute-done | bytes 131104 | tf_op jit(solution)/shard_map/ppermute | solution.py:88
  26.6 9.3 %collective-permute-done.4 = bf16[32,2,1024]{2,0,1:T(8,128)(2,1)S(1)} collective-permute-done((bf16[32,2,1024]{2,0,1:T(8,128)(2,1)S(1)}, bf16[32,2,1024]{2,0,1:T(8,128)(2,1)S(1)}, u32[]{:S(2)}, u32[]{:S(2)}) %collective-permute-start.4) | collective-permute-done | bytes 131104 | tf_op jit(solution)/shard_map/ppermute | solution.py:88
  36.0 0.6 gather_fusion
  36.6 1.1 copy.30
  37.7 0.0 all-reduce.4.cloned.1.call-start
  37.8 58.3 %all-gather.2.cloned.1.call-done = bf16[1024,2,1024]{2,0,1:T(8,128)(2,1)} async-done(((bf16[256,2,1024]{2,0,1:T(8,128)(2,1)}), bf16[1024,2,1024]{2,0,1:T(8,128)(2,1)}) %all-gather.2.cloned.1.call-update) | async-done | bytes 4194320 | tf_op jit(solution)/shard_map/all_gather | solution.py:95
  96.0 4.6 %fusion.4 = f32[4,2,2,64,1024]{4,3,2,0,1:T(8,128)S(1)} fusion(bf16[1024,2,1024]{2,0,1:T(8,128)(2,1)} %all-gather.2.cloned.1.call-done, bf16[4,2,64,1024]{3,2,1,0:T(8,128)(2,1)S(1)} %copy-done.1), kind=kOutput, calls=%fused_computation.5 | convolution fusion | flops 2147483648 | bytes 9437184 | tf_op jit(solution)/shard_map/pcg,fekg->fcekp/dot_general | solution.py:51
  100.6 0.1 fusion.15
  100.7 0.2 fusion.17
  100.9 1.5 pad_maximum_fusion
  102.5 0.0 all-reduce.4.cloned.1.call-update
  102.5 0.0 all-reduce.6.cloned.1.call-start
  102.5 0.6 copy-done.5
  103.1 0.2 dynamic-update-slice
  103.4 40.1 %all-reduce = s32[1024]{0:T(1024)S(1)} all-reduce(s32[1024]{0:T(1024)S(1)} %dynamic-update-slice), channel_id=1, replica_groups=mesh['freq'=4,'band'=8] {'freq','band'}, use_global_device_ids=true, to_apply=%add | all-reduce | flops 1024 | bytes 8192
  143.5 0.1 select_reduce_fusion
  143.6 0.1 fusion.30
  143.7 24.7 %all-reduce.4.cloned.1.call-done = f32[4,2,64,1024]{3,2,0,1:T(8,128)} async-done(((f32[4,2,64,1024]{3,2,0,1:T(8,128)}), f32[4,2,64,1024]{3,2,0,1:T(8,128)}) %all-reduce.4.cloned.1.call-update) | async-done | bytes 2097168 | tf_op jit(solution)/shard_map/psum | solution.py:98
  168.4 1.8 multiply_convert_fusion
  170.3 0.1 slice_negate_fusion
  170.4 0.2 maximum_bitcast_fusion
  170.6 1.9 copy-done.4
  172.4 2.3 fusion.8
  174.8 0.6 fusion.19
  175.4 0.6 fusion.20
  176.1 0.6 fusion.14
  176.7 0.6 fusion.13
  177.3 0.7 maximum_multiply_fusion
  178.1 55.2 %all-reduce.6.cloned.1.call-done = f32[4,2,64,64]{2,3,0,1:T(8,128)} async-done(((f32[4,2,64,64]{2,3,0,1:T(8,128)}), f32[4,2,64,64]{2,3,0,1:T(8,128)}) %all-reduce.6.cloned.1.call-update) | async-done | bytes 131088 | tf_op jit(solution)/shard_map/psum | solution.py:111
  233.3 1.8 copy.36
  (32 shorter events, 0.2 us)
Async XLA Ops:
  7.2 88.9 %all-gather.2.cloned.1.call-start = ((), (), s32[]{:S(2)}) async-start(), calls=%async_computation | async-start | bytes 5242880 | tf_op jit(solution)/shard_map/all_gather | solution.py:95
  11.6 6.9 %collective-permute-start = (bf16[32,2,1024]{2,0,1:T(8,128)(2,1)S(1)}, bf16[32,2,1024]{2,0,1:T(8,128)(2,1)S(1)}, u32[]{:S(2)}, u32[]{:S(2)}) collective-permute-start(bf16[32,2,1024]{2,0,1:T(8,128)(2,1)S(1)} %bitcast.126), channel_id=1, source_target_pairs={{0,1},{1,0},{2,3},{3,2},{4,5},{5,4},{6,7},{7,6},{8,9},{9,8},{10,11... | collective-permute-start | bytes 393224 | tf_op jit(solution)/shard_map/ppermute | solution.py:88
  12.2 9.9 %collective-permute-start.1 = (bf16[32,2,1024]{2,0,1:T(8,128)(2,1)S(1)}, bf16[32,2,1024]{2,0,1:T(8,128)(2,1)S(1)}, u32[]{:S(2)}, u32[]{:S(2)}) collective-permute-start(bf16[32,2,1024]{2,0,1:T(8,128)(2,1)S(1)} %bitcast.125), channel_id=1, source_target_pairs={{0,2},{1,3},{2,0},{3,1},{4,6},{5,7},{6,4},{7,5},{8,10},{9,11},{10,... | collective-permute-start | bytes 393224 | tf_op jit(solution)/shard_map/ppermute | solution.py:88
  15.0 11.6 %collective-permute-start.2 = (bf16[32,2,1024]{2,0,1:T(8,128)(2,1)S(1)}, bf16[32,2,1024]{2,0,1:T(8,128)(2,1)S(1)}, u32[]{:S(2)}, u32[]{:S(2)}) collective-permute-start(bf16[32,2,1024]{2,0,1:T(8,128)(2,1)S(1)} %bitcast.123), channel_id=1, source_target_pairs={{0,3},{1,2},{2,1},{3,0},{4,7},{5,6},{6,5},{7,4},{8,11},{9,10},{10,... | collective-permute-start | bytes 393224 | tf_op jit(solution)/shard_map/ppermute | solution.py:88
  15.2 11.3 %collective-permute-start.3 = (bf16[32,2,1024]{2,0,1:T(8,128)(2,1)S(1)}, bf16[32,2,1024]{2,0,1:T(8,128)(2,1)S(1)}, u32[]{:S(2)}, u32[]{:S(2)}) collective-permute-start(bf16[32,2,1024]{2,0,1:T(8,128)(2,1)S(1)} %bitcast.122), channel_id=1, source_target_pairs={{0,4},{1,5},{2,6},{3,7},{4,0},{5,1},{6,2},{7,3},{8,12},{9,13},{10,... | collective-permute-start | bytes 393224 | tf_op jit(solution)/shard_map/ppermute | solution.py:88
  18.1 17.8 %collective-permute-start.4 = (bf16[32,2,1024]{2,0,1:T(8,128)(2,1)S(1)}, bf16[32,2,1024]{2,0,1:T(8,128)(2,1)S(1)}, u32[]{:S(2)}, u32[]{:S(2)}) collective-permute-start(bf16[32,2,1024]{2,0,1:T(8,128)(2,1)S(1)} %bitcast.121), channel_id=1, source_target_pairs={{0,5},{1,4},{2,7},{3,6},{4,1},{5,0},{6,3},{7,2},{8,13},{9,12},{10,... | collective-permute-start | bytes 393224 | tf_op jit(solution)/shard_map/ppermute | solution.py:88
  18.5 17.4 %collective-permute-start.5 = (bf16[32,2,1024]{2,0,1:T(8,128)(2,1)S(1)}, bf16[32,2,1024]{2,0,1:T(8,128)(2,1)S(1)}, u32[]{:S(2)}, u32[]{:S(2)}) collective-permute-start(bf16[32,2,1024]{2,0,1:T(8,128)(2,1)S(1)} %bitcast.124), channel_id=1, source_target_pairs={{0,6},{1,7},{2,4},{3,5},{4,2},{5,3},{6,0},{7,1},{8,14},{9,15},{10,... | collective-permute-start | bytes 393224 | tf_op jit(solution)/shard_map/ppermute | solution.py:88
  22.1 13.8 %collective-permute-start.6 = (bf16[32,2,1024]{2,0,1:T(8,128)(2,1)S(1)}, bf16[32,2,1024]{2,0,1:T(8,128)(2,1)S(1)}, u32[]{:S(2)}, u32[]{:S(2)}) collective-permute-start(bf16[32,2,1024]{2,0,1:T(8,128)(2,1)S(1)} %bitcast.120), channel_id=1, source_target_pairs={{0,7},{1,6},{2,5},{3,4},{4,3},{5,2},{6,1},{7,0},{8,15},{9,14},{10,... | collective-permute-start | bytes 393224 | tf_op jit(solution)/shard_map/ppermute | solution.py:88
  36.6 59.4 %copy-start.1 = (bf16[4,2,64,1024]{3,2,1,0:T(8,128)(2,1)S(1)}, bf16[4,2,64,1024]{3,2,1,0:T(8,128)(2,1)}, u32[]{:S(2)}) copy-start(bf16[4,2,64,1024]{3,2,1,0:T(8,128)(2,1)} %param.7) | copy-start | bytes 3145732
  37.7 130.7 %all-reduce.4.cloned.1.call-start = ((), (), s32[]{:S(2)}) async-start(), calls=%async_computation.1 | async-start | bytes 4194304 | tf_op jit(solution)/shard_map/psum | solution.py:98
  102.5 0.7 copy-start.5
  102.5 0.7 copy-start.6
  102.5 41.0 %copy-start.2 = (f32[32]{0:T(128)S(1)}, f32[32]{0:T(128)}, u32[]{:S(2)}) copy-start(f32[32]{0:T(128)} %param.9) | copy-start | bytes 388
  102.5 41.0 %copy-start.3 = (f32[32]{0:T(128)S(1)}, f32[32]{0:T(128)}, u32[]{:S(2)}) copy-start(f32[32]{0:T(128)} %param.10) | copy-start | bytes 388
  102.5 130.8 %all-reduce.6.cloned.1.call-start = ((), (), s32[]{:S(2)}) async-start(), calls=%async_computation.2 | async-start | bytes 524288 | tf_op jit(solution)/shard_map/psum | solution.py:111
  170.3 2.2 copy-start.4
  174.8 1.9 copy-start
Sparse Core Ops, SparseCore 0:
  37.8 58.1 all-gather.1
  102.6 65.7 all-reduce.3
  178.2 55.0 all-reduce.5
